TPU v7x, 32 devices: a whole 2x2x4 slice. The times are simulated.
32 devices in a mesh: gx: 8 (over y, x, core), gy: 4 (over z).
Axes of the slice: x: 2, y: 2, z: 4, core: 2. Of those that a mesh axis runs over, the one named last changes fastest.
Arguments:
- spectrum: float32 [192, 160, 1080], P('gx', 'gy'), may hold values from 0.05 to 1
- adjoint_in: float32 [192, 160, 1080], P('gx', 'gy'), may hold values from 0 to 2
- current_x: float32 [192, 160], P('gx', 'gy'), may hold values from -0.08 to 0.08
- current_y: float32 [192, 160], P('gx', 'gy'), may hold values from -0.08 to 0.08
- wind_x: float32 [192, 160], P('gx', 'gy'), may hold values from -4 to 4
- wind_y: float32 [192, 160], P('gx', 'gy'), may hold values from -4 to 4
- land_mask: int32 [192, 160], P('gx', 'gy'), may hold values from 0 to 1, as said below
- ice_mask: int32 [192, 160], P('gx', 'gy'), may hold values from 0 to 1, as said below
- group_speed: float32 [30], replicated, may hold values from 0.1 to 0.4
- growth_rate: float32 [30], replicated, may hold values from 0.1 to 1
- dissipation: float32 [30], replicated, may hold values from 0.3 to 3
Outputs:
- adjoint_spectrum: float32 [192, 160, 1080], P('gx', 'gy')
Inputs may be any that keep to these rules, and one draw needn't show every extreme that they name: `land_mask`: 1 marks land, 0 sea. `ice_mask`: 1 marks sea ice, 0 open water.
All inputs are finite; a program needn't handle non-finite values.
Results may differ from a plain program's by a relative error of at most 0.0001.
Values sent between devices are 32-bit elements; how exact they have to be, the bound alone decides.
A program may use at most 128 MiB of HBM per device.

v0:
```python
import math

import jax
import jax.numpy as jnp
from jax import lax
from jax.sharding import PartitionSpec as P

DIRS = 36


def with_halo(block, sides, width, periodic):
    for axis, dim in sides:
        count = lax.axis_size(axis)
        forward = [(i, i + 1) for i in range(count - 1)]
        if periodic:
            forward.append((count - 1, 0))
        backward = [(target, source) for source, target in forward]
        low = lax.ppermute(
            lax.slice_in_dim(block, block.shape[dim] - width, None, axis=dim), axis, forward
        )
        high = lax.ppermute(lax.slice_in_dim(block, 0, width, axis=dim), axis, backward)
        block = jnp.concatenate([low, block, high], axis=dim)
    return block


def face_lon(statics, cosine, speeds):
    sea_mask = statics[..., 2]
    opened = sea_mask[:-1] * sea_mask[1:]
    drift_avg = 0.5 * (statics[:-1, :, 0] + statics[1:, :, 0])
    courant = opened[..., None] * (speeds * cosine + drift_avg[..., None])
    return (jnp.maximum(courant, 0.0), jnp.minimum(courant, 0.0))


def face_lat(statics, sine_bin, speeds):
    sea_mask = statics[..., 2]
    opened = sea_mask[:, :-1] * sea_mask[:, 1:]
    drift_avg = 0.5 * (statics[:, :-1, 1] + statics[:, 1:, 1])
    courant = opened[..., None] * (speeds * sine_bin + drift_avg[..., None])
    return (jnp.maximum(courant, 0.0), jnp.minimum(courant, 0.0))


def advect(lon_field, lat_field, lon_statics, lat_statics, tables):
    lon_plus, lon_minus = face_lon(lon_statics, tables[0], tables[2])
    lat_plus, lat_minus = face_lat(lat_statics, tables[1], tables[2])
    lon_flux = lon_plus * lon_field[:-1] + lon_minus * lon_field[1:]
    lat_flux = lat_plus * lat_field[:, :-1] + lat_minus * lat_field[:, 1:]
    centre = lon_field[1:-1]
    advected = centre - (lon_flux[1:] - lon_flux[:-1]) - (lat_flux[:, 1:] - lat_flux[:, :-1])
    return (advected, lon_plus, lon_minus, lat_plus, lat_minus)


def source_adjoint(advected, incoming, sea_mask, wind_east, wind_north, ice_free, tables):
    cosine, sine_bin, growth, damping = (tables[0], tables[1], tables[3], tables[4])
    project = wind_east[..., None] * cosine + wind_north[..., None] * sine_bin
    gained = 1.0 + growth * jnp.maximum(project, 0.0) * ice_free[..., None]
    energy = jnp.sum(advected, axis=2, keepdims=True) / advected.shape[2]
    damped = 1.0 + damping * energy * advected
    weighted = incoming * gained / (damped * damped)
    coupling = jnp.sum(weighted * damping * advected * advected, axis=2, keepdims=True)
    return sea_mask[..., None] * (weighted - coupling / advected.shape[2])


def body(
    spectrum,
    adjoint_in,
    current_x,
    current_y,
    wind_x,
    wind_y,
    land_mask,
    ice_mask,
    group_speed,
    growth_rate,
    dissipation,
):
    directions = DIRS
    angles = 2.0 * math.pi / directions * (jnp.arange(directions, dtype=jnp.float32) + 0.5)
    per_dir = group_speed.shape[0]
    cosine = jnp.repeat(jnp.cos(angles), per_dir)
    sine_bin = jnp.repeat(jnp.sin(angles), per_dir)
    tables = (
        cosine,
        sine_bin,
        jnp.tile(group_speed, directions),
        jnp.tile(growth_rate, directions),
        jnp.tile(dissipation, directions),
    )
    sea_mask = (1 - land_mask).astype(jnp.float32)
    ice_free = (1 - ice_mask).astype(jnp.float32)
    statics = jnp.stack([current_x, current_y, sea_mask], axis=2)
    lon_field, lon_statics = (
        with_halo(spectrum, (("gx", 0),), 1, True),
        with_halo(statics, (("gx", 0),), 1, True),
    )
    lat_field, lat_statics = (
        with_halo(spectrum, (("gy", 1),), 1, False),
        with_halo(statics, (("gy", 1),), 1, False),
    )
    advected, lon_plus, lon_minus, lat_plus, lat_minus = advect(
        lon_field, lat_field, lon_statics, lat_statics, tables
    )
    sensitivity = source_adjoint(advected, adjoint_in, sea_mask, wind_x, wind_y, ice_free, tables)
    retained = sensitivity * (
        1.0 - lon_plus[1:] + lon_minus[:-1] - lat_plus[:, 1:] + lat_minus[:, :-1]
    )
    westward = lon_plus[:-1] * sensitivity
    eastward = -lon_minus[1:] * sensitivity
    southward = lat_plus[:, :-1] * sensitivity
    northward = -lat_minus[:, 1:] * sensitivity
    lon_rims = jnp.concatenate([westward[:1], eastward[-1:]], axis=0)
    lat_rims = jnp.concatenate([southward[:, :1], northward[:, -1:]], axis=1)
    back_lon = with_halo(lon_rims, (("gx", 0),), 1, True)
    back_lat = with_halo(lat_rims, (("gy", 1),), 1, False)
    zero_row = jnp.zeros_like(sensitivity[:1])
    zero_col = jnp.zeros_like(sensitivity[:, :1])
    result = (
        retained
        + jnp.concatenate([westward[1:], zero_row], axis=0)
        + jnp.concatenate([zero_row, eastward[:-1]], axis=0)
    )
    result = (
        result
        + jnp.concatenate([southward[:, 1:], zero_col], axis=1)
        + jnp.concatenate([zero_col, northward[:, :-1]], axis=1)
    )
    result = result.at[0].add(back_lon[0]).at[-1].add(back_lon[-1])
    result = result.at[:, 0].add(back_lat[:, 0]).at[:, -1].add(back_lat[:, -1])
    return result


def solution(mesh):
    placed = (
        P("gx", "gy", None),
        P("gx", "gy", None),
        P("gx", "gy"),
        P("gx", "gy"),
        P("gx", "gy"),
        P("gx", "gy"),
        P("gx", "gy"),
        P("gx", "gy"),
        P(),
        P(),
        P(),
    )
    return jax.shard_map(
        body, mesh=mesh, in_specs=placed, out_specs=P("gx", "gy", None), check_vma=False
    )
```

profile of v0, /device:TPU:0, one launch (start us, length us, event | category | flops | bytes accessed | tf_op | source)
XLA Modules:
  0.0 114.1 jit_solution(3339073274403516975)
XLA Ops:
  0.0 0.7 subtract_convert_fusion.1
  0.7 0.7 pad_maximum_fusion.18
  1.5 0.5 collective-permute-start
  2.0 2.9 %collective-permute-start.1 = (f32[1,40,3]{1,0,2:T(1,128)S(1)}, f32[1,40,3]{1,0,2:T(1,128)S(1)}, u32[]{:S(2)}, u32[]{:S(2)}) collective-permute-start(f32[1,40,3]{1,0,2:T(1,128)S(1)} %get-tuple-element.71), channel_id=1, source_target_pairs={{4,0},{8,4},{12,8},{16,12},{20,16},{24,20},{28,24},{0,28},{5,1},{9... | collective-permute-start | bytes 1448 | tf_op jit(solution)/shard_map/ppermute | solution.py:21
  4.9 0.7 pad_maximum_fusion
  5.6 0.1 fusion.33
  5.7 4.2 %collective-permute-start.4 = (f32[24,1,3]{1,0,2:T(8,128)S(1)}, f32[24,1,3]{1,0,2:T(8,128)S(1)}, u32[]{:S(2)}, u32[]{:S(2)}) collective-permute-start(f32[24,1,3]{1,0,2:T(8,128)S(1)} %get-tuple-element.72), channel_id=1, source_target_pairs={{0,1},{1,2},{2,3},{4,5},{5,6},{6,7},{8,9},{9,10},{10,11},{12,13},{... | collective-permute-start | bytes 872 | tf_op jit(solution)/shard_map/ppermute | solution.py:18
  9.9 1.3 %collective-permute-start.5 = (f32[24,1,3]{1,0,2:T(8,128)S(1)}, f32[24,1,3]{1,0,2:T(8,128)S(1)}, u32[]{:S(2)}, u32[]{:S(2)}) collective-permute-start(f32[24,1,3]{1,0,2:T(8,128)S(1)} %get-tuple-element.73), channel_id=1, source_target_pairs={{1,0},{2,1},{3,2},{5,4},{6,5},{7,6},{9,8},{10,9},{11,10},{13,12},{... | collective-permute-start | bytes 872 | tf_op jit(solution)/shard_map/ppermute | solution.py:21
  11.2 1.6 %fusion.32 = (f32[24,1,1080]{2,1,0:T(1,128)S(1)}, f32[24,1,1080]{2,1,0:T(1,128)S(1)}) fusion(f32[24,40,1080]{2,1,0:T(8,128)} %param.19), kind=kLoop, calls=%fused_computation.80 | loop fusion | bytes 414720 | tf_op jit(solution)/shard_map/slice | solution.py:21
  12.8 4.6 %collective-permute-start.6 = (f32[24,1,1080]{2,0,1:T(8,128)S(1)}, f32[24,1,1080]{2,0,1:T(8,128)S(1)}, u32[]{:S(2)}, u32[]{:S(2)}) collective-permute-start(f32[24,1,1080]{2,0,1:T(8,128)S(1)} %copy.39), channel_id=1, source_target_pairs={{0,1},{1,2},{2,3},{4,5},{5,6},{6,7},{8,9},{9,10},{10,11},{12,13},{... | collective-permute-start | bytes 311048 | tf_op jit(solution)/shard_map/ppermute | solution.py:18
  17.5 1.0 fusion.31
  18.5 0.7 subtract_convert_fusion
  19.2 0.1 broadcast_in_dim.11
  19.3 0.1 mul.198
  19.4 0.1 broadcast_in_dim.10
  19.5 0.1 mul.194
  19.6 0.7 tile.10
  20.2 0.1 tile.11
  20.3 0.7 tile.8
  21.0 0.1 mul.189
  21.1 0.7 tile.9
  21.8 0.1 mul.205
  21.9 0.0 collective-permute-done.4
  21.9 1.3 %collective-permute-start.7 = (f32[24,1,1080]{2,0,1:T(8,128)S(1)}, f32[24,1,1080]{2,0,1:T(8,128)S(1)}, u32[]{:S(2)}, u32[]{:S(2)}) collective-permute-start(f32[24,1,1080]{2,0,1:T(8,128)S(1)} %copy.40), channel_id=1, source_target_pairs={{1,0},{2,1},{3,2},{5,4},{6,5},{7,6},{9,8},{10,9},{11,10},{13,12},{... | collective-permute-start | bytes 311048 | tf_op jit(solution)/shard_map/ppermute | solution.py:21
  23.2 0.1 collective-permute-start.3
  23.3 0.1 fusion.25
  23.4 0.1 slice_multiply_fusion.2
  23.5 0.9 fusion.24
  24.3 0.5 collective-permute-start.2
  24.9 0.8 fusion.21
  25.7 0.0 slice-start
  25.7 0.1 copy.32
  25.8 2.7 %collective-permute-done.7 = f32[24,1,1080]{2,0,1:T(8,128)S(1)} collective-permute-done((f32[24,1,1080]{2,0,1:T(8,128)S(1)}, f32[24,1,1080]{2,0,1:T(8,128)S(1)}, u32[]{:S(2)}, u32[]{:S(2)}) %collective-permute-start.7) | collective-permute-done | bytes 103712 | tf_op jit(solution)/shard_map/ppermute | solution.py:21
  28.6 0.1 copy.34
  28.7 0.0 slice-start.1
  28.7 10.7 %fusion = (f32[24,41,1080]{2,1,0:T(8,128)}, f32[24,41,1080]{2,1,0:T(8,128)}, f32[24,41,1080]{2,1,0:T(8,128)}) fusion(f32[24,40,1080]{2,1,0:T(8,128)} %param.19, f32[24,1,1080]{2,1,0:T(1,128)S(1)} %copy.32, f32[24,1,1080]{2,1,0:T(1,128)S(1)} %copy.34, f32[24,41]{1,0:T(8,128)S(1)} %fusion.24, f32[1080]{0:T(1024)S(1)} %get-tuple-element.80, ...), kind=kLoop, calls=%fused_computation.2 | loop fusion | flops 9564480 | bytes 17119392 | tf_op jit(solution)/shard_map/add | solution.py:46
  39.5 2.7 %fusion.3 = (f32[25,40,1080]{2,1,0:T(8,128)S(1)}, f32[25,40,1080]{2,1,0:T(8,128)S(1)}, f32[25,40,1080]{2,1,0:T(8,128)S(1)}) fusion(f32[24,40,1080]{2,1,0:T(8,128)S(1)} %bitcast.14, f32[1,40,1080]{2,1,0:T(8,128)S(1)} %collective-permute-done.2, f32[1,40,1080]{2,1,0:T(8,128)S(1)} %collective-permute-done.3, f32[25,40]{1,0:T(8,128)S(1)} %get-tuple-element.69, ...), kind=kLoop, calls=%fused_computation.8 | loop fusion | flops 9720000 | bytes 17465120 | tf_op jit(solution)/shard_map/add | solution.py:45
  42.2 0.0 copy-start.1
  42.2 0.0 copy-start.2
  42.2 7.6 %fusion.29 = (f32[24,40]{1,0:T(8,128)S(1)}, f32[24,40,1080]{2,1,0:T(8,128)}) fusion(f32[24,41,1080]{2,1,0:T(8,128)} %get-tuple-element.74, f32[24,40,1080]{2,1,0:T(8,128)S(1)} %bitcast.14, f32[25,40,1080]{2,1,0:T(8,128)S(1)} %get-tuple-element.65), kind=kLoop, calls=%fused_computation.78 | loop fusion | flops 5183040 | bytes 24887040 | tf_op jit(solution)/shard_map/reduce_sum | solution.py:56
  49.9 5.8 %fusion.6 = (f32[24,40]{1,0:T(8,128)S(1)}, f32[24,40,1080]{2,1,0:T(8,128)S(1)}) fusion(f32[24,40,1080]{2,1,0:T(8,128)} %get-tuple-element.56, f32[1080]{0:T(1024)S(1)} %mul.205, f32[24,40]{1,0:T(8,128)S(1)} %broadcast_multiply_fusion.1, f32[24,40,1080]{2,1,0:T(8,128)} %param.20, f32[24,40]{1,0:T(8,128)S(1)} %subtract_convert_fusion, f32[1080]{0:T(1024)S(1)} %mul.198, ...), kind=kLoop, calls=%fused_computation.13 | loop fusion | flops 17624640 | bytes 12478080 | tf_op jit(solution)/shard_map/reduce_sum | solution.py:59
  55.7 0.0 copy-done
  55.7 9.8 %slice_multiply_fusion.1 = (f32[24,40,1080]{2,1,0:T(8,128)}, f32[24,40,1080]{2,1,0:T(8,128)}, f32[24,40,1080]{2,1,0:T(8,128)}, f32[24,40,1080]{2,1,0:T(8,128)}) fusion(f32[25,40,1080]{2,1,0:T(8,128)S(1)} %get-tuple-element.67, f32[24,40,1080]{2,1,0:T(8,128)S(1)} %get-tuple-element.54, f32[24,40]{1,0:T(8,128)S(1)} %broadcast_multiply_fusion, ...), kind=kLoop, calls=%fused_computation.19 | loop fusion | flops 8294400 | bytes 37332480 | tf_op jit(solution)/shard_map/mul | solution.py:106
  65.5 1.4 %slice.286 = f32[24,1,1080]{2,1,0:T(1,128)S(1)} slice(f32[24,40,1080]{2,1,0:T(8,128)} %get-tuple-element.59), slice={[0:24], [0:1], [0:1080]} | slice | bytes 207360 | tf_op jit(solution)/shard_map/slice | solution.py:111
  66.9 0.0 slice-start.5
  66.9 4.8 %slice.276 = f32[24,39,1080]{2,1,0:T(8,128)} slice(f32[24,40,1080]{2,1,0:T(8,128)} %get-tuple-element.59), slice={[0:24], [1:40], [0:1080]} | slice | bytes 8087040 | tf_op jit(solution)/shard_map/slice | solution.py:123
  71.7 2.4 %slice.272 = f32[23,40,1080]{2,1,0:T(8,128)} slice(f32[24,40,1080]{2,1,0:T(8,128)S(1)} %bitcast.19), slice={[1:24], [0:40], [0:1080]} | slice | bytes 7948800 | tf_op jit(solution)/shard_map/slice | solution.py:118
  74.1 1.2 %slice-done.2 = s8[4194304]{0:T(1024)(128)(4,1)S(1)} async-done(((s8[4423680]{0:T(1024)(128)(4,1)}), s8[4194304]{0:T(1024)(128)(4,1)S(1)}, s32[]{:S(2)}) %slice-start.2) | async-done | bytes 4194328
  75.4 0.0 slice-done.3
  75.4 2.3 %slice.274 = f32[23,40,1080]{2,1,0:T(8,128)} slice(f32[24,40,1080]{2,1,0:T(8,128)S(1)} %bitcast.17), slice={[0:23], [0:40], [0:1080]} | slice | bytes 7948800 | tf_op jit(solution)/shard_map/slice | solution.py:119
  77.7 0.7 copy.37
  78.3 1.3 %slice.284 = f32[24,1,1080]{2,1,0:T(1,128)S(1)} slice(f32[24,40,1080]{2,1,0:T(8,128)} %get-tuple-element.60), slice={[0:24], [39:40], [0:1080]} | slice | bytes 207360 | tf_op jit(solution)/shard_map/slice | solution.py:111
  79.6 0.7 copy.35
  80.3 4.1 %collective-permute-start.10 = (f32[24,1,1080]{2,0,1:T(8,128)}, f32[24,1,1080]{2,0,1:T(8,128)}, u32[]{:S(2)}, u32[]{:S(2)}) collective-permute-start(f32[24,1,1080]{2,0,1:T(8,128)} %copy.35), channel_id=1, source_target_pairs={{0,1},{1,2},{2,3},{4,5},{5,6},{6,7},{8,9},{9,10},{10,11},{12,13},{... | collective-permute-start | bytes 311048 | tf_op jit(solution)/shard_map/ppermute | solution.py:18
  84.4 1.3 %collective-permute-start.11 = (f32[24,1,1080]{2,0,1:T(8,128)}, f32[24,1,1080]{2,0,1:T(8,128)}, u32[]{:S(2)}, u32[]{:S(2)}) collective-permute-start(f32[24,1,1080]{2,0,1:T(8,128)} %copy.37), channel_id=1, source_target_pairs={{1,0},{2,1},{3,2},{5,4},{6,5},{7,6},{9,8},{10,9},{11,10},{13,12},{... | collective-permute-start | bytes 311048 | tf_op jit(solution)/shard_map/ppermute | solution.py:21
  85.7 0.1 collective-permute-start.8
  85.7 2.6 %collective-permute-start.9 = (f32[1,40,1080]{2,1,0:T(8,128)S(1)}, f32[1,40,1080]{2,1,0:T(8,128)S(1)}, u32[]{:S(2)}, u32[]{:S(2)}) collective-permute-start(f32[1,40,1080]{2,1,0:T(8,128)S(1)} %slice.282), channel_id=1, source_target_pairs={{4,0},{8,4},{12,8},{16,12},{20,16},{24,20},{28,24},{0,28},{5,1},{9... | collective-permute-start | bytes 518408 | tf_op jit(solution)/shard_map/ppermute | solution.py:21
  88.4 13.7 %fusion.13 = f32[24,40,1080]{2,1,0:T(8,128)} fusion(f32[24,41,1080]{2,1,0:T(8,128)} %get-tuple-element.75, f32[24,41,1080]{2,1,0:T(8,128)} %get-tuple-element.76, f32[25,40,1080]{2,1,0:T(8,128)S(1)} %get-tuple-element.66, f32[25,40,1080]{2,1,0:T(8,128)} %copy-done, f32[24,39,1080]{2,1,0:T(8,128)} %bitcast.15, f32[24,39,1080]{2,1,0:T(8,128)} %slice.276, ...), kind=kLoop, calls=%fused_computation.25 | loop fusion | flops 11404800 | bytes 40926720 | tf_op jit(solution)/shard_map/add | solution.py:122
  102.1 1.6 %fusion.17 = f32[24,40,1080]{2,1,0:T(8,128)} fusion(f32[24,40,1080]{2,1,0:T(8,128)} %fusion.13, f32[1,40,1080]{2,1,0:T(8,128)S(1)} %collective-permute-done.8), kind=kLoop, calls=%fused_computation.38 | loop fusion | flops 43200 | bytes 541440 | tf_op jit(solution)/shard_map/scatter-add | solution.py:126
  103.7 1.6 %fusion.16 = f32[24,40,1080]{2,1,0:T(8,128)} fusion(f32[24,40,1080]{2,1,0:T(8,128)} %fusion.17, f32[1,40,1080]{2,1,0:T(8,128)S(1)} %collective-permute-done.9), kind=kLoop, calls=%fused_computation.36 | loop fusion | flops 43200 | bytes 541440 | tf_op jit(solution)/shard_map/scatter-add | solution.py:126
  105.3 1.3 %slice_add_fusion.5 = f32[24,1,1080]{2,1,0:T(1,128)S(1)} fusion(f32[24,40,1080]{2,1,0:T(8,128)} %fusion.16, f32[24,1,1080]{2,0,1:T(8,128)} %collective-permute-done.10), kind=kLoop, calls=%fused_computation.40 | loop fusion | flops 25920 | bytes 311040 | tf_op jit(solution)/shard_map/add | solution.py:127
  106.6 3.1 %scatter-add.16 = f32[24,40,1080]{2,1,0:T(8,128)} dynamic-update-slice(f32[24,40,1080]{2,1,0:T(8,128)} %fusion.16, f32[24,1,1080]{2,1,0:T(1,128)S(1)} %slice_add_fusion.5, s32[]{:T(128)} %constant.126.clone.1, s32[]{:T(128)} %constant.126.clone.1, s32[]{:T(128)} %constant.126.clone.1) | dynamic-update-slice | bytes 207364 | tf_op jit(solution)/shard_map/scatter-add | solution.py:127
  109.7 1.3 %slice_add_fusion.4 = f32[24,1,1080]{2,1,0:T(1,128)S(1)} fusion(f32[24,40,1080]{2,1,0:T(8,128)} %scatter-add.16, f32[24,1,1080]{2,0,1:T(8,128)} %collective-permute-done.11), kind=kLoop, calls=%fused_computation.39 | loop fusion | flops 25920 | bytes 311040 | tf_op jit(solution)/shard_map/add | solution.py:127
  111.0 3.1 %scatter-add.19 = f32[24,40,1080]{2,1,0:T(8,128)} dynamic-update-slice(f32[24,40,1080]{2,1,0:T(8,128)} %scatter-add.16, f32[24,1,1080]{2,1,0:T(1,128)S(1)} %slice_add_fusion.4, s32[]{:T(128)} %constant.126.clone.1, s32[]{:T(128)} %constant.128.clone.1, s32[]{:T(128)} %constant.126.clone.1) | dynamic-update-slice | bytes 207364 | tf_op jit(solution)/shard_map/scatter-add | solution.py:127
  (32 shorter events, 0.2 us)
Async XLA Ops:
  1.5 22.9 %collective-permute-start = (f32[1,40,3]{1,0,2:T(1,128)S(1)}, f32[1,40,3]{1,0,2:T(1,128)S(1)}, u32[]{:S(2)}, u32[]{:S(2)}) collective-permute-start(f32[1,40,3]{1,0,2:T(1,128)S(1)} %get-tuple-element.70), channel_id=1, source_target_pairs={{0,4},{4,8},{8,12},{12,16},{16,20},{20,24},{24,28},{28,0},{1,5},{5... | collective-permute-start | bytes 1448 | tf_op jit(solution)/shard_map/ppermute | solution.py:18
  2.0 22.9 %collective-permute-start.1 = (f32[1,40,3]{1,0,2:T(1,128)S(1)}, f32[1,40,3]{1,0,2:T(1,128)S(1)}, u32[]{:S(2)}, u32[]{:S(2)}) collective-permute-start(f32[1,40,3]{1,0,2:T(1,128)S(1)} %get-tuple-element.71), channel_id=1, source_target_pairs={{4,0},{8,4},{12,8},{16,12},{20,16},{24,20},{28,24},{0,28},{5,1},{9... | collective-permute-start | bytes 1448 | tf_op jit(solution)/shard_map/ppermute | solution.py:21
  5.7 16.2 %collective-permute-start.4 = (f32[24,1,3]{1,0,2:T(8,128)S(1)}, f32[24,1,3]{1,0,2:T(8,128)S(1)}, u32[]{:S(2)}, u32[]{:S(2)}) collective-permute-start(f32[24,1,3]{1,0,2:T(8,128)S(1)} %get-tuple-element.72), channel_id=1, source_target_pairs={{0,1},{1,2},{2,3},{4,5},{5,6},{6,7},{8,9},{9,10},{10,11},{12,13},{... | collective-permute-start | bytes 872 | tf_op jit(solution)/shard_map/ppermute | solution.py:18
  9.9 13.3 %collective-permute-start.5 = (f32[24,1,3]{1,0,2:T(8,128)S(1)}, f32[24,1,3]{1,0,2:T(8,128)S(1)}, u32[]{:S(2)}, u32[]{:S(2)}) collective-permute-start(f32[24,1,3]{1,0,2:T(8,128)S(1)} %get-tuple-element.73), channel_id=1, source_target_pairs={{1,0},{2,1},{3,2},{5,4},{6,5},{7,6},{9,8},{10,9},{11,10},{13,12},{... | collective-permute-start | bytes 872 | tf_op jit(solution)/shard_map/ppermute | solution.py:21
  12.8 12.9 %collective-permute-start.6 = (f32[24,1,1080]{2,0,1:T(8,128)S(1)}, f32[24,1,1080]{2,0,1:T(8,128)S(1)}, u32[]{:S(2)}, u32[]{:S(2)}) collective-permute-start(f32[24,1,1080]{2,0,1:T(8,128)S(1)} %copy.39), channel_id=1, source_target_pairs={{0,1},{1,2},{2,3},{4,5},{5,6},{6,7},{8,9},{9,10},{10,11},{12,13},{... | collective-permute-start | bytes 311048 | tf_op jit(solution)/shard_map/ppermute | solution.py:18
  21.9 6.6 %collective-permute-start.7 = (f32[24,1,1080]{2,0,1:T(8,128)S(1)}, f32[24,1,1080]{2,0,1:T(8,128)S(1)}, u32[]{:S(2)}, u32[]{:S(2)}) collective-permute-start(f32[24,1,1080]{2,0,1:T(8,128)S(1)} %copy.40), channel_id=1, source_target_pairs={{1,0},{2,1},{3,2},{5,4},{6,5},{7,6},{9,8},{10,9},{11,10},{13,12},{... | collective-permute-start | bytes 311048 | tf_op jit(solution)/shard_map/ppermute | solution.py:21
  23.2 16.2 %collective-permute-start.3 = (f32[1,40,1080]{2,1,0:T(8,128)S(1)}, f32[1,40,1080]{2,1,0:T(8,128)S(1)}, u32[]{:S(2)}, u32[]{:S(2)}) collective-permute-start(f32[1,40,1080]{2,1,0:T(8,128)S(1)} %get-tuple-element.61), channel_id=1, source_target_pairs={{4,0},{8,4},{12,8},{16,12},{20,16},{24,20},{28,24},{0,28},{5,1},{9... | collective-permute-start | bytes 518408 | tf_op jit(solution)/shard_map/ppermute | solution.py:21
  24.3 15.1 %collective-permute-start.2 = (f32[1,40,1080]{2,1,0:T(8,128)S(1)}, f32[1,40,1080]{2,1,0:T(8,128)S(1)}, u32[]{:S(2)}, u32[]{:S(2)}) collective-permute-start(f32[1,40,1080]{2,1,0:T(8,128)S(1)} %get-tuple-element.62), channel_id=1, source_target_pairs={{0,4},{4,8},{8,12},{12,16},{16,20},{20,24},{24,28},{28,0},{1,5},{5... | collective-permute-start | bytes 518408 | tf_op jit(solution)/shard_map/ppermute | solution.py:18
  25.7 13.7 %slice-start = ((s8[4423680]{0:T(1024)(128)(4,1)}), s8[4194304]{0:T(1024)(128)(4,1)S(1)}, s32[]{:S(2)}) async-start(s8[4423680]{0:T(1024)(128)(4,1)} %bitcast.13), calls=%async_computation | async-start | bytes 8388608
  28.7 10.8 %slice-start.1 = ((s8[4423680]{0:T(1024)(128)(4,1)}), s8[229376]{0:T(1024)(128)(4,1)S(1)}, s32[]{:S(2)}) async-start(s8[4423680]{0:T(1024)(128)(4,1)} %bitcast.13), calls=%async_computation.1 | async-start | bytes 458752
  42.2 13.5 %copy-start = (f32[25,40,1080]{2,1,0:T(8,128)}, f32[25,40,1080]{2,1,0:T(8,128)S(1)}, u32[]{:S(2)}) copy-start(f32[25,40,1080]{2,1,0:T(8,128)S(1)} %get-tuple-element.67) | copy-start | bytes 12960004
  42.2 7.7 %copy-start.1 = (f32[24,40]{1,0:T(8,128)S(1)}, f32[24,40]{1,0:T(8,128)}, u32[]{:S(2)}) copy-start(f32[24,40]{1,0:T(8,128)} %param.24) | copy-start | bytes 11524
  42.2 7.7 %copy-start.2 = (f32[24,40]{1,0:T(8,128)S(1)}, f32[24,40]{1,0:T(8,128)}, u32[]{:S(2)}) copy-start(f32[24,40]{1,0:T(8,128)} %param.23) | copy-start | bytes 11524
  65.5 6.2 %slice-start.4 = ((s8[4423680]{0:T(1024)(128)(4,1)}), s8[4194304]{0:T(1024)(128)(4,1)S(1)}, s32[]{:S(2)}) async-start(s8[4423680]{0:T(1024)(128)(4,1)} %bitcast.18), calls=%async_computation.4 | async-start | bytes 8388608
  66.9 4.8 %slice-start.5 = ((s8[4423680]{0:T(1024)(128)(4,1)}), s8[229376]{0:T(1024)(128)(4,1)S(1)}, s32[]{:S(2)}) async-start(s8[4423680]{0:T(1024)(128)(4,1)} %bitcast.18), calls=%async_computation.5 | async-start | bytes 458752
  71.7 3.7 %slice-start.2 = ((s8[4423680]{0:T(1024)(128)(4,1)}), s8[4194304]{0:T(1024)(128)(4,1)S(1)}, s32[]{:S(2)}) async-start(s8[4423680]{0:T(1024)(128)(4,1)} %bitcast.16), calls=%async_computation.2 | async-start | bytes 8388608
  71.7 3.7 %slice-start.3 = ((s8[4423680]{0:T(1024)(128)(4,1)}), s8[229376]{0:T(1024)(128)(4,1)S(1)}, s32[]{:S(2)}) async-start(s8[4423680]{0:T(1024)(128)(4,1)} %bitcast.16), calls=%async_computation.3 | async-start | bytes 458752
  80.3 25.1 %collective-permute-start.10 = (f32[24,1,1080]{2,0,1:T(8,128)}, f32[24,1,1080]{2,0,1:T(8,128)}, u32[]{:S(2)}, u32[]{:S(2)}) collective-permute-start(f32[24,1,1080]{2,0,1:T(8,128)} %copy.35), channel_id=1, source_target_pairs={{0,1},{1,2},{2,3},{4,5},{5,6},{6,7},{8,9},{9,10},{10,11},{12,13},{... | collective-permute-start | bytes 311048 | tf_op jit(solution)/shard_map/ppermute | solution.py:18
  84.4 25.3 %collective-permute-start.11 = (f32[24,1,1080]{2,0,1:T(8,128)}, f32[24,1,1080]{2,0,1:T(8,128)}, u32[]{:S(2)}, u32[]{:S(2)}) collective-permute-start(f32[24,1,1080]{2,0,1:T(8,128)} %copy.37), channel_id=1, source_target_pairs={{1,0},{2,1},{3,2},{5,4},{6,5},{7,6},{9,8},{10,9},{11,10},{13,12},{... | collective-permute-start | bytes 311048 | tf_op jit(solution)/shard_map/ppermute | solution.py:21
  85.7 16.4 %collective-permute-start.8 = (f32[1,40,1080]{2,1,0:T(8,128)S(1)}, f32[1,40,1080]{2,1,0:T(8,128)S(1)}, u32[]{:S(2)}, u32[]{:S(2)}) collective-permute-start(f32[1,40,1080]{2,1,0:T(8,128)S(1)} %slice.280), channel_id=1, source_target_pairs={{0,4},{4,8},{8,12},{12,16},{16,20},{20,24},{24,28},{28,0},{1,5},{5... | collective-permute-start | bytes 518408 | tf_op jit(solution)/shard_map/ppermute | solution.py:18
  85.7 18.0 %collective-permute-start.9 = (f32[1,40,1080]{2,1,0:T(8,128)S(1)}, f32[1,40,1080]{2,1,0:T(8,128)S(1)}, u32[]{:S(2)}, u32[]{:S(2)}) collective-permute-start(f32[1,40,1080]{2,1,0:T(8,128)S(1)} %slice.282), channel_id=1, source_target_pairs={{4,0},{8,4},{12,8},{16,12},{20,16},{24,20},{28,24},{0,28},{5,1},{9... | collective-permute-start | bytes 518408 | tf_op jit(solution)/shard_map/ppermute | solution.py:21
where the time goes:
time: 115 us; the launch traced here: 114 us
  other arithmetic  61 us (53%)
  local copies, waits for them, and re-layouts  26.5 us (23%)
  starting transfers between devices  23.5 us (20%)
  waiting for transfers between devices  2.76 us (2%)
    ppermute x6, starting transfers between devices, with_halo(): lax.ppermute(lax.slice_in_dim(block, block.shape[dim] - width, None, axis...  14 us
    add x1, other arithmetic, body(): result + jnp.concatenate([southward[:, 1:], zero_col], axis=1)  13.7 us
    add x1, other arithmetic, advect(): lat_flux = lat_plus * lat_field[:, :-1] + lat_minus * lat_field[:, 1:]  10.7 us
    mul x1, other arithmetic, body(): westward = lon_plus[:-1] * sensitivity  9.81 us
    ppermute x6, starting transfers between devices, with_halo(): lax.ppermute(lax.slice_in_dim(block, 0, width, axis=dim), axis, backward)  9.49 us
    reduce_sum x1, other arithmetic, source_adjoint(): energy = jnp.sum(advected, axis=2, keepdims=True) / advected.shape[2]  7.64 us
    scatter-add x2, local copies, waits for them, and re-layouts, body(): result = result.at[:, 0].add(back_lat[:, 0]).at[:, -1].add(back_lat[:, -1])  6.19 us
    reduce_sum x1, other arithmetic, source_adjoint(): jnp.sum(weighted * damping * advected * advected, axis=2, keepdims=True)  5.79 us
  transfers between devices with their start and end apart: 12, of which 1 were waited for; matrix products, arithmetic and copies ran while one was open for 36% of the time, Pallas kernels for 0%

commit v1 on v0

v1 whole, which is shorter than its diff:
```python
import functools
import math

import jax
import jax.numpy as jnp
import numpy as np
from jax import lax
from jax.experimental import pallas as pl
from jax.experimental.pallas import tpu as pltpu
from jax.sharding import PartitionSpec as P

DIRS = 36
LANES = 128
ANY = pl.BlockSpec(memory_space=pl.ANY)
VMEM = pl.BlockSpec(memory_space=pltpu.VMEM)


def lane_chunks(bins):
    return [(s, min(LANES, bins - s)) for s in range(0, bins, LANES)]


def up(block, last):
    return jnp.concatenate([block[1:], last], axis=0)


def down(block, first):
    return jnp.concatenate([first, block[:-1]], axis=0)


def spread(cells, stats, table, count):
    for k in range(count):
        turned = table[k][:cells, :]

        def one(i, carry, k=k, turned=turned):
            column = pltpu.roll(turned, LANES - i, axis=1)[:, 0:1]
            stats[k, i] = jnp.broadcast_to(column, (cells, LANES))
            return carry

        lax.fori_loop(1, stats.shape[1], one, 0)
        stats[k, 0] = jnp.broadcast_to(turned[:, 0:1], (cells, LANES))


def forward_kernel(
    nx, ny,
    spectrum, adjoint, cx, cy, wx, wy, land, ice, speed, growth, diss, trig,
    sens_out, lon_out, lat_out, turned_out, table_out,
    sp, adj, sens, lat, near_f, near_i, ext, face, turned, stats, flux, work, lat_s, params,
    local_sem, out_sem, far_send, far_recv,
):
    gx, gy = lax.axis_index("gx"), lax.axis_index("gy")
    rows, cells, bins = adjoint.shape
    east, west = lax.rem(gx + 1, nx), lax.rem(gx + nx - 1, nx)
    has_north, has_south = gy < ny - 1, gy > 0
    chunks = lane_chunks(bins)
    pad = stats.shape[2]

    barrier = pltpu.get_barrier_semaphore()
    for axis, where in (("gx", east), ("gx", west)):
        pl.semaphore_signal(barrier, inc=1, device_id={axis: where}, device_id_type=pl.DeviceIdType.MESH)

    @pl.when(has_north)
    def _():
        pl.semaphore_signal(barrier, inc=1, device_id={"gy": gy + 1}, device_id_type=pl.DeviceIdType.MESH)

    @pl.when(has_south)
    def _():
        pl.semaphore_signal(barrier, inc=1, device_id={"gy": gy - 1}, device_id_type=pl.DeviceIdType.MESH)

    half = rows // 2
    loads = []
    for n, (src, dst, off) in enumerate(((spectrum, sp, 1), (adjoint, adj, 0))):
        for m in range(2):
            loads.append(
                pltpu.make_async_copy(
                    src.at[pl.ds(m * half, half)], dst.at[pl.ds(m * half + off, half)], local_sem.at[2 * n + m]
                )
            )
    for copy in loads:
        copy.start()

    def far(src, dst, n, axis, where):
        return pltpu.make_async_remote_copy(
            src_ref=src, dst_ref=dst, send_sem=far_send.at[n], recv_sem=far_recv.at[n],
            device_id={axis: where}, device_id_type=pl.DeviceIdType.MESH,
        )

    to_east = [
        far(cx, near_f.at[0], 0, "gx", east),
        far(land, near_i.at[0], 1, "gx", east),
        far(spectrum.at[rows - 1], sp.at[0], 2, "gx", east),
    ]
    to_west = [
        far(cx, near_f.at[1], 3, "gx", west),
        far(land, near_i.at[1], 4, "gx", west),
        far(spectrum.at[0], sp.at[rows + 1], 5, "gx", west),
    ]
    to_north = [
        far(cy, near_f.at[2], 6, "gy", gy + 1),
        far(land, near_i.at[2], 7, "gy", gy + 1),
        far(spectrum.at[:, pl.ds(cells - 1, 1), :], lat.at[0], 8, "gy", gy + 1),
    ]
    to_south = [
        far(cy, near_f.at[3], 9, "gy", gy - 1),
        far(land, near_i.at[3], 10, "gy", gy - 1),
        far(spectrum.at[:, pl.ds(0, 1), :], lat.at[1], 11, "gy", gy - 1),
    ]

    @pl.when(jnp.logical_not(has_south))
    def _():
        lat[0] = jnp.zeros(lat.shape[1:], jnp.float32)

    @pl.when(jnp.logical_not(has_north))
    def _():
        lat[1] = jnp.zeros(lat.shape[1:], jnp.float32)

    pl.semaphore_wait(barrier, 2 + has_north.astype(jnp.int32) + has_south.astype(jnp.int32))

    def each_lat(method, first=0, last=3):
        @pl.when(has_north)
        def _():
            for copy in to_north[first:last]:
                getattr(copy, method)()

        @pl.when(has_south)
        def _():
            for copy in to_south[first:last]:
                getattr(copy, method)()

    def lat_arrives(first, last):
        @pl.when(has_south)
        def _():
            for copy in to_north[first:last]:
                copy.wait_recv()

        @pl.when(has_north)
        def _():
            for copy in to_south[first:last]:
                copy.wait_recv()

    each_lat("start", 2, 3)
    for copy in to_east[2:] + to_west[2:]:
        copy.start()
    for copy in to_east[:2] + to_west[:2]:
        copy.start()
    each_lat("start", 0, 2)

    freqs = speed.shape[1]
    params[...] = jnp.zeros(params.shape, jnp.float32)
    params[0:1, 0:freqs] = speed[...]
    params[1:2, 0:freqs] = growth[...]
    params[2:3, 0:freqs] = diss[...]
    spots = lax.rem(lax.broadcasted_iota(jnp.int32, (params.shape[1], bins), 1), freqs)
    hot = (spots == lax.broadcasted_iota(jnp.int32, (params.shape[1], bins), 0)).astype(jnp.float32)
    by_bin = jnp.dot(params[...], hot, precision=lax.Precision.HIGHEST, preferred_element_type=jnp.float32)
    cosine, sine = trig[0:1], trig[1:2]
    table_out[0:1] = by_bin[0:1] * cosine
    table_out[1:2] = by_bin[0:1] * sine
    table_out[2:3] = by_bin[1:2] * cosine
    table_out[3:4] = by_bin[1:2] * sine
    table_out[4:5] = by_bin[2:3]
    table = table_out

    for copy in to_east[:2] + to_west[:2]:
        copy.wait_recv()
    lat_arrives(0, 2)
    ext[...] = jnp.zeros(ext.shape, jnp.float32)
    sea_of = lambda mask: (1 - mask).astype(jnp.float32)
    ext[0, 0:1, 0:cells] = near_f[0, rows - 1 : rows]
    ext[0, 1 : rows + 1, 0:cells] = cx[...]
    ext[0, rows + 1 : rows + 2, 0:cells] = near_f[1, 0:1]
    ext[1, 0:1, 0:cells] = sea_of(near_i[0, rows - 1 : rows])
    ext[1, 1 : rows + 1, 0:cells] = sea_of(land[...])
    ext[1, rows + 1 : rows + 2, 0:cells] = sea_of(near_i[1, 0:1])
    ext[2, 0:rows, 0:cells] = cy[...]
    ext[3, 0:rows, 0:cells] = sea_of(land[...])
    ext[4, 0:rows, 0:cells] = near_f[2]
    ext[5, 0:rows, 0:cells] = sea_of(near_i[2])
    ext[6, 0:rows, 0:cells] = near_f[3]
    ext[7, 0:rows, 0:cells] = sea_of(near_i[3])
    face[...] = jnp.zeros(face.shape, jnp.float32)
    opened = ext[1, 0 : rows + 1] * ext[1, 1 : rows + 2]
    face[0, 0 : rows + 1] = opened
    face[1, 0 : rows + 1] = opened * (0.5 * (ext[0, 0 : rows + 1] + ext[0, 1 : rows + 2]))
    tall = ext.shape[1]
    lane = lax.broadcasted_iota(jnp.int32, (tall, LANES), 1)

    def pair(own, south, north):
        mine = jnp.where(lane == cells, pltpu.roll(own, cells, axis=1), own)
        other = jnp.where(lane == cells - 1, pltpu.roll(north, cells - 1, axis=1), pltpu.roll(own, LANES - 1, axis=1))
        other = jnp.where(lane == cells, pltpu.roll(south, 1, axis=1), other)
        return mine, other

    sea_a, sea_b = pair(ext[3], ext[5], ext[7])
    cy_a, cy_b = pair(ext[2], ext[4], ext[6])
    closed = jnp.logical_or(
        jnp.logical_and(lane == cells, jnp.logical_not(has_south)),
        jnp.logical_and(lane == cells - 1, jnp.logical_not(has_north)),
    )
    opened = sea_a * sea_b
    face[2, 0:tall] = jnp.where(closed, 0.0, opened)
    face[3, 0:tall] = jnp.where(closed, 0.0, opened * (0.5 * (cy_a + cy_b)))
    ice_free = sea_of(ice[...])
    face[4, 0:rows, 0:cells] = wx[...] * ice_free
    face[5, 0:rows, 0:cells] = wy[...] * ice_free
    face[6, 0:rows, 0:cells] = sea_of(land[...])
    for k in range(7):
        turned[k] = face[k].T
    turned_out[...] = turned[0:4, 0:pad]
    spread(pad, stats, turned, 7)

    for copy in loads:
        copy.wait()
    for copy in to_east[2:] + to_west[2:]:
        copy.wait_recv()
    lat_arrives(2, 3)

    def lon_flux(f, s, w):
        courant = stats[0, f, 0:cells, 0:w] * table[0:1, s : s + w] + stats[1, f, 0:cells, 0:w]
        return courant * jnp.where(courant > 0, sp[f, :, s : s + w], sp[f + 1, :, s : s + w])

    lon_send = [
        far(sens.at[rows - 1], lon_out.at[0], 12, "gx", east),
        far(sens.at[0], lon_out.at[1], 13, "gx", west),
    ]
    lat_north = [far(lat_s.at[1, pl.ds(m * half, half)], lat_out.at[0, pl.ds(m * half, half)], 14 + m, "gy", gy + 1) for m in range(2)]
    lat_south = [far(lat_s.at[0, pl.ds(m * half, half)], lat_out.at[1, pl.ds(m * half, half)], 16 + m, "gy", gy - 1) for m in range(2)]

    def lat_send(m):
        @pl.when(has_north)
        def _():
            lat_north[m].start()

        @pl.when(has_south)
        def _():
            lat_south[m].start()

    def send_row(i):
        return pltpu.make_async_copy(sens.at[i], sens_out.at[i], out_sem.at[i])

    def row(k, carry):
        i = lax.rem(k + rows - 1, rows)

        @pl.when(k < 2)
        def _():
            for s, w in chunks:
                flux[:, s : s + w] = lon_flux(i, s, w)

        @pl.when(k == 2)
        def _():
            for copy in lon_send:
                copy.start()

        @pl.when(k == half + 2)
        def _():
            lat_send(0)

        energy = jnp.zeros((cells, 1), jnp.float32)
        total = jnp.zeros((cells, LANES), jnp.float32)
        for s, w in chunks:
            own = sp[i + 1, :, s : s + w]
            fx = lon_flux(i + 1, s, w)
            fx_low = flux[:, s : s + w]
            sin_row = table[1:2, s : s + w]
            courant = stats[2, i, 0:cells, 0:w] * sin_row + stats[3, i, 0:cells, 0:w]
            fy = courant * jnp.where(courant > 0, own, up(own, lat[1, i, :, s : s + w]))
            low = stats[2, i, cells : cells + 1, 0:w] * sin_row + stats[3, i, cells : cells + 1, 0:w]
            fy_low = down(fy, low * jnp.where(low > 0, lat[0, i, :, s : s + w], own[0:1]))
            advected = own - (fx - fx_low) - (fy - fy_low)
            flux[:, s : s + w] = fx
            work[:, s : s + w] = advected
            if w == LANES:
                total = total + advected
            else:
                energy = energy + jnp.sum(advected, axis=1, keepdims=True)
        energy = (energy + jnp.sum(total, axis=1, keepdims=True)) * (1.0 / bins)
        energy = jnp.broadcast_to(energy, (cells, LANES))
        coupling = jnp.zeros((cells, 1), jnp.float32)
        total = jnp.zeros((cells, LANES), jnp.float32)
        for s, w in chunks:
            advected = work[:, s : s + w]
            blow = stats[4, i, 0:cells, 0:w] * table[2:3, s : s + w] + stats[5, i, 0:cells, 0:w] * table[3:4, s : s + w]
            gain = 1.0 + jnp.maximum(blow, 0.0)
            scaled = table[4:5, s : s + w] * advected
            damp = 1.0 + energy[:, 0:w] * scaled
            weighted = adj[i, :, s : s + w] * gain / (damp * damp)
            sens[i, :, s : s + w] = weighted
            term = weighted * scaled * advected
            if w == LANES:
                total = total + term
            else:
                coupling = coupling + jnp.sum(term, axis=1, keepdims=True)
        coupling = (coupling + jnp.sum(total, axis=1, keepdims=True)) * (1.0 / bins)
        coupling = jnp.broadcast_to(coupling, (cells, LANES))
        for s, w in chunks:
            value = stats[6, i, 0:cells, 0:w] * (sens[i, :, s : s + w] - coupling[:, 0:w])
            sens[i, :, s : s + w] = value
            lat_s[0, i, :, s : s + w] = value[0:1]
            lat_s[1, i, :, s : s + w] = value[cells - 1 : cells]

        @pl.when(k > 0)
        def _():
            send_row(lax.rem(k + rows - 2, rows)).start()

        return carry

    lax.fori_loop(0, rows, row, 0)
    lat_send(1)
    send_row(rows - 2).start()

    fill = [pltpu.make_async_copy(lat.at[m], lat_out.at[m], local_sem.at[m]) for m in range(2)]
    for m, there in ((0, has_south), (1, has_north)):
        @pl.when(jnp.logical_not(there))
        def _(m=m):
            fill[m].start()

    for copy in to_east + to_west:
        copy.wait_send()
    each_lat("wait_send")
    for copy in lon_send:
        copy.wait()

    @pl.when(has_north)
    def _():
        for copy in lat_north:
            copy.wait_send()
        for copy in lat_south:
            copy.wait_recv()

    @pl.when(has_south)
    def _():
        for copy in lat_south:
            copy.wait_send()
        for copy in lat_north:
            copy.wait_recv()

    for m, there in ((0, has_south), (1, has_north)):
        @pl.when(jnp.logical_not(there))
        def _(m=m):
            fill[m].wait()

    def finish(i, carry):
        send_row(i).wait()
        return carry

    lax.fori_loop(0, rows, finish, 0)


def transpose_kernel(
    sens, lon, lat, turned, table, out,
    ext, stats, held, done, in_sem, out_sem,
):
    rows, cells, bins = sens.shape
    chunks = lane_chunks(bins)
    pad = stats.shape[2]
    groups = in_sem.shape[0] - 2
    size = rows // groups
    edges = [pltpu.make_async_copy(lon.at[m], ext.at[m * (rows + 1)], in_sem.at[groups + m]) for m in range(2)]
    part = lambda g: pltpu.make_async_copy(sens.at[pl.ds(g * size, size)], ext.at[pl.ds(g * size + 1, size)], in_sem.at[g])
    edges[0].start()
    for g in range(groups):
        part(g).start()
    edges[1].start()
    spread(pad, stats, turned, 4)
    edges[0].wait()
    part(0).wait()

    def lon_face(f, s, w):
        return stats[0, f, 0:cells, 0:w] * table[0:1, s : s + w] + stats[1, f, 0:cells, 0:w]

    for s, w in chunks:
        held[:, s : s + w] = jnp.minimum(lon_face(0, s, w), 0.0) * (ext[1, :, s : s + w] - ext[0, :, s : s + w])

    send = lambda i: pltpu.make_async_copy(done.at[i], out.at[i], out_sem.at[i])

    def row(i, carry):
        @pl.when(jnp.logical_and(lax.rem(i, size) == size - 1, i < rows - 1))
        def _():
            part(i // size + 1).wait()

        @pl.when(i == rows - 1)
        def _():
            edges[1].wait()

        for s, w in chunks:
            own = ext[i + 1, :, s : s + w]
            step = ext[i + 2, :, s : s + w] - own
            courant = lon_face(i + 1, s, w)
            value = own + held[:, s : s + w] + jnp.maximum(courant, 0.0) * step
            held[:, s : s + w] = jnp.minimum(courant, 0.0) * step
            sin_row = table[1:2, s : s + w]
            courant = stats[2, i, 0:cells, 0:w] * sin_row + stats[3, i, 0:cells, 0:w]
            step = up(own, lat[1, i, :, s : s + w]) - own
            value = value + jnp.maximum(courant, 0.0) * step
            low = stats[2, i, cells : cells + 1, 0:w] * sin_row + stats[3, i, cells : cells + 1, 0:w]
            low = jnp.minimum(low, 0.0) * (own[0:1] - lat[0, i, :, s : s + w])
            done[i, :, s : s + w] = value + down(jnp.minimum(courant, 0.0) * step, low)

        @pl.when(i > 0)
        def _():
            send(i - 1).start()

        return carry

    lax.fori_loop(0, rows, row, 0)
    send(rows - 1).start()

    def finish(i, carry):
        send(i).wait()
        return carry

    lax.fori_loop(0, rows, finish, 0)


def round_up(value, step):
    return (value + step - 1) // step * step


def body(nx, ny, spectrum, adjoint_in, cx, cy, wx, wy, land, ice, speed, growth, diss):
    rows, cells, bins = spectrum.shape
    freqs = speed.shape[0]
    angles = 2.0 * math.pi / DIRS * (np.arange(DIRS) + 0.5)
    trig = np.stack([np.repeat(np.cos(angles), freqs), np.repeat(np.sin(angles), freqs)]).astype(np.float32)
    pad = round_up(cells + 1, 8)
    tall = round_up(rows + 2, 8)
    f32 = jnp.float32
    dma = pltpu.SemaphoreType.DMA
    shape = jax.ShapeDtypeStruct
    sens, lon, lat, turned, table = pl.pallas_call(
        functools.partial(forward_kernel, nx, ny),
        out_shape=(
            shape((rows, cells, bins), f32),
            shape((2, cells, bins), f32),
            shape((2, rows, 1, bins), f32),
            shape((4, pad, LANES), f32),
            shape((8, bins), f32),
        ),
        in_specs=[ANY, ANY] + [VMEM] * 10,
        out_specs=(ANY, ANY, ANY, VMEM, VMEM),
        scratch_shapes=[
            pltpu.VMEM((rows + 2, cells, bins), f32),
            pltpu.VMEM((rows, cells, bins), f32),
            pltpu.VMEM((rows, cells, bins), f32),
            pltpu.VMEM((2, rows, 1, bins), f32),
            pltpu.VMEM((4, rows, cells), f32),
            pltpu.VMEM((4, rows, cells), jnp.int32),
            pltpu.VMEM((8, tall, LANES), f32),
            pltpu.VMEM((7, LANES, LANES), f32),
            pltpu.VMEM((7, LANES, LANES), f32),
            pltpu.VMEM((7, rows + 1, pad, LANES), f32),
            pltpu.VMEM((cells, bins), f32),
            pltpu.VMEM((cells, bins), f32),
            pltpu.VMEM((2, rows, 1, bins), f32),
            pltpu.VMEM((8, round_up(freqs, 8)), f32),
            dma((4,)),
            dma((rows,)),
            dma((18,)),
            dma((18,)),
        ],
        compiler_params=pltpu.CompilerParams(
            collective_id=0, has_side_effects=True, vmem_limit_bytes=40 * 2**20
        ),
        name="forward",
    )(spectrum, adjoint_in, cx, cy, wx, wy, land, ice,
      speed.reshape(1, -1), growth.reshape(1, -1), diss.reshape(1, -1), jnp.asarray(trig))
    groups = max(g for g in (1, 2, 3, 4, 6) if rows % g == 0)
    return pl.pallas_call(
        transpose_kernel,
        out_shape=shape((rows, cells, bins), f32),
        in_specs=[ANY, ANY, VMEM, VMEM, VMEM],
        out_specs=ANY,
        scratch_shapes=[
            pltpu.VMEM((rows + 2, cells, bins), f32),
            pltpu.VMEM((4, rows + 1, pad, LANES), f32),
            pltpu.VMEM((cells, bins), f32),
            pltpu.VMEM((rows, cells, bins), f32),
            dma((groups + 2,)),
            dma((rows,)),
        ],
        compiler_params=pltpu.CompilerParams(vmem_limit_bytes=32 * 2**20),
        name="transpose",
    )(sens, lon, lat, turned, table)


def solution(mesh):
    grid = P("gx", "gy")
    field = P("gx", "gy", None)
    return jax.shard_map(
        functools.partial(body, mesh.shape["gx"], mesh.shape["gy"]),
        mesh=mesh,
        in_specs=(field, field) + (grid,) * 6 + (P(), P(), P()),
        out_specs=field,
        check_vma=False,
    )
```

time: 115 us -> 85.5 us (0.74)
  Pallas kernels: 0 us -> 73.4 us
  other arithmetic: 61 us -> 0 us
  starting transfers between devices: 23.5 us -> 0 us
  local copies, waits for them, and re-layouts: 26.5 us -> 11.4 us
  waiting for transfers between devices: 2.76 us -> 0 us
    pallas_call x0 -> x2, Pallas kernels: none -> 73.4 us  [the longest x1 52.6 us: body(): pl.pallas_call(functools.partial(forward_kernel, nx, ny), out_shape=(shap...]
    add x6 -> x0, other arithmetic: 30.6 us -> none  [the longest x1 13.7 us: body(): result + jnp.concatenate([southward[:, 1:], zero_col], axis=1)]
    ppermute x12 -> x0, starting transfers between devices: 23.5 us -> none  [the longest x6 14 us: with_halo(): lax.ppermute(lax.slice_in_dim(block, block.shape[dim] - width, None, axis...]
    slice x12 -> x0, local copies, waits for them, and re-layouts: 16.2 us -> none  [the longest x1 4.77 us: body(): southward[:, 1:]]
    reduce_sum x2 -> x0, other arithmetic: 13.4 us -> none  [the longest x1 7.64 us: source_adjoint(): energy = jnp.sum(advected, axis=2, keepdims=True) / advected.shape[2]]
    mul x4 -> x0, other arithmetic: 10.7 us -> none  [the longest x1 9.81 us: body(): westward = lon_plus[:-1] * sensitivity]
    unnamed x20 -> x24, local copies, waits for them, and re-layouts: 1.33 us -> 11.4 us
    scatter-add x2 -> x0, local copies, waits for them, and re-layouts: 6.19 us -> none  [body(): result = result.at[:, 0].add(back_lat[:, 0]).at[:, -1].add(back_lat[:, -1])]
  transfers between devices with their start and end apart: 12 -> 0, of which waited for: 1 -> 0; matrix products, arithmetic and copies ran while one was open for 36% -> 0% of each run, Pallas kernels for 0% -> 0%
where the time goes in v1:
time: 85.5 us; the launch traced here: 84.8 us
  Pallas kernels  73.4 us (86%)
  local copies, waits for them, and re-layouts  11.4 us (13%)
    pallas_call x1, Pallas kernels, body(): pl.pallas_call(functools.partial(forward_kernel, nx, ny), out_shape=(shap...  52.6 us
    pallas_call x1, Pallas kernels, body(): pl.pallas_call(transpose_kernel, out_shape=shape((rows, cells, bins), f32...  20.8 us
    unnamed x24, local copies, waits for them, and re-layouts  11.4 us

profile of v1, /device:TPU:0, one launch (start us, length us, event | category | flops | bytes accessed | tf_op | source)
XLA Modules:
  0.0 84.8 jit_solution(4255685953759540494)
XLA Ops:
  0.0 0.0 copy-start
  0.0 2.3 %copy-done = f32[24,40,1080]{2,1,0:T(8,128)S(1)} copy-done((f32[24,40,1080]{2,1,0:T(8,128)S(1)}, f32[24,40,1080]{2,1,0:T(8,128)}, u32[]{:S(2)}) %copy-start) | copy-done | bytes 4147224
  2.3 0.0 copy-start.1
  2.3 2.3 %copy-done.1 = f32[24,40,1080]{2,1,0:T(8,128)S(1)} copy-done((f32[24,40,1080]{2,1,0:T(8,128)S(1)}, f32[24,40,1080]{2,1,0:T(8,128)}, u32[]{:S(2)}) %copy-start.1) | copy-done | bytes 4147224
  4.5 0.0 copy-start.2
  4.5 0.7 copy-done.2
  5.2 0.0 copy-start.3
  5.2 0.7 copy-done.3
  5.9 0.0 copy-start.4
  5.9 0.7 copy-done.4
  6.6 0.0 copy-start.5
  6.6 0.7 copy-done.5
  7.3 0.0 copy-start.6
  7.3 0.7 copy-done.6
  8.0 0.0 copy-start.7
  8.0 0.7 copy-done.7
  8.8 0.0 copy-start.8
  8.8 0.7 copy-done.8
  9.5 0.0 copy-start.9
  9.5 0.7 copy-done.9
  10.1 0.0 copy-start.10
  10.1 0.7 copy-done.10
  10.8 0.0 copy-start.11
  10.8 0.7 copy-done.11
  11.4 52.6 %forward.1 = (f32[24,40,1080]{2,1,0:T(8,128)S(1)}, f32[2,40,1080]{2,1,0:T(8,128)S(1)}, f32[2,24,1,1080]{3,2,1,0:T(1,128)S(1)}, f32[4,48,128]{2,1,0:T(8,128)S(1)}, f32[8,1080]{1,0:T(8,128)S(1)}) custom-call(f32[24,40,1080]{2,1,0:T(8,128)S(1)} %copy-done, f32[24,40,1080]{2,1,0:T(8,128)S(1)} %copy-done.1, f32[24,40]{1,0:T(8,128)S(1)} %copy-done.2, ...), custom_call_target="tpu_custom_call" | custom-call | tf_op jit(solution)/shard_map/forward/pallas_call | solution.py:428
  64.0 20.8 %transpose.1 = f32[24,40,1080]{2,1,0:T(8,128)} custom-call(f32[24,40,1080]{2,1,0:T(8,128)S(1)} %get-tuple-element.10.sens, f32[2,40,1080]{2,1,0:T(8,128)S(1)} %get-tuple-element.11.lon, f32[2,24,1,1080]{3,2,1,0:T(1,128)S(1)} %get-tuple-element.12.lat, f32[4,48,128]{2,1,0:T(8,128)S(1)} %get-tuple-element.13.turned, f32[8,1080]{1,0:T(8,128)S(1)} %get-tuple-element.14.table), custom_call_target="tpu_custom_call" | custom-call | tf_op jit(solution)/shard_map/transpose/pallas_call | solution.py:466
Async XLA Ops:
  0.0 2.3 %copy-start = (f32[24,40,1080]{2,1,0:T(8,128)S(1)}, f32[24,40,1080]{2,1,0:T(8,128)}, u32[]{:S(2)}) copy-start(f32[24,40,1080]{2,1,0:T(8,128)} %spectrum.1) | copy-start | bytes 12441604
  2.3 2.3 %copy-start.1 = (f32[24,40,1080]{2,1,0:T(8,128)S(1)}, f32[24,40,1080]{2,1,0:T(8,128)}, u32[]{:S(2)}) copy-start(f32[24,40,1080]{2,1,0:T(8,128)} %adjoint.1) | copy-start | bytes 12441604
  4.5 0.7 copy-start.2
  5.2 0.7 copy-start.3
  5.9 0.7 copy-start.4
  6.6 0.7 copy-start.5
  7.3 0.7 copy-start.6
  8.0 0.7 copy-start.7
  8.8 0.7 copy-start.8
  9.5 0.7 copy-start.9
  10.1 0.7 copy-start.10
  10.8 0.7 copy-start.11

commit v2 on v1

--- a/solution.py
+++ b/solution.py
@@ -11,7 +11,7 @@
 
 DIRS = 36
 LANES = 128
-ANY = pl.BlockSpec(memory_space=pl.ANY)
+HBM = pl.BlockSpec(memory_space=pltpu.HBM)
 VMEM = pl.BlockSpec(memory_space=pltpu.VMEM)
 
 
@@ -36,16 +36,16 @@
             stats[k, i] = jnp.broadcast_to(column, (cells, LANES))
             return carry
 
-        lax.fori_loop(1, stats.shape[1], one, 0)
+        lax.fori_loop(1, stats.shape[1], one, 0, unroll=4)
         stats[k, 0] = jnp.broadcast_to(turned[:, 0:1], (cells, LANES))
 
 
 def forward_kernel(
     nx, ny,
-    spectrum, adjoint, cx, cy, wx, wy, land, ice, speed, growth, diss, trig,
-    sens_out, lon_out, lat_out, turned_out, table_out,
-    sp, adj, sens, lat, near_f, near_i, ext, face, turned, stats, flux, work, lat_s, params,
-    local_sem, out_sem, far_send, far_recv,
+    spectrum, adjoint, cx_h, cy_h, wx_h, wy_h, land_h, ice_h, speed_h, growth_h, diss_h, trig_h,
+    sens, lat_out, stats, table,
+    sp, adj, lat, rim, near_f, near_i, mine_f, mine_i, coeffs, trig, ext, face, turned, flux, work, lat_s, params,
+    local_sem, far_send, far_recv,
 ):
     gx, gy = lax.axis_index("gx"), lax.axis_index("gy")
     rows, cells, bins = adjoint.shape
@@ -67,6 +67,19 @@
         pl.semaphore_signal(barrier, inc=1, device_id={"gy": gy - 1}, device_id_type=pl.DeviceIdType.MESH)
 
     half = rows // 2
+    small = []
+    cx, cy, wx, wy = (mine_f.at[m] for m in range(4))
+    land, ice = (mine_i.at[m] for m in range(2))
+    speed, growth, diss = (coeffs.at[m] for m in range(3))
+    pairs = (
+        (spectrum.at[:, pl.ds(0, 1), :], rim.at[0]), (spectrum.at[:, pl.ds(cells - 1, 1), :], rim.at[1]),
+        (cx_h, cx), (cy_h, cy), (land_h, land), (ice_h, ice), (wx_h, wx), (wy_h, wy),
+        (speed_h, speed), (growth_h, growth), (diss_h, diss), (trig_h, trig),
+    )
+    for m, (src, dst) in enumerate(pairs):
+        small.append(pltpu.make_async_copy(src, dst, local_sem.at[4 + m]))
+    for copy in small:
+        copy.start()
     loads = []
     for n, (src, dst, off) in enumerate(((spectrum, sp, 1), (adjoint, adj, 0))):
         for m in range(2):
@@ -85,24 +98,24 @@
         )
 
     to_east = [
-        far(cx, near_f.at[0], 0, "gx", east),
-        far(land, near_i.at[0], 1, "gx", east),
+        far(cx_h, near_f.at[0], 0, "gx", east),
+        far(land_h, near_i.at[0], 1, "gx", east),
         far(spectrum.at[rows - 1], sp.at[0], 2, "gx", east),
     ]
     to_west = [
-        far(cx, near_f.at[1], 3, "gx", west),
-        far(land, near_i.at[1], 4, "gx", west),
+        far(cx_h, near_f.at[1], 3, "gx", west),
+        far(land_h, near_i.at[1], 4, "gx", west),
         far(spectrum.at[0], sp.at[rows + 1], 5, "gx", west),
     ]
     to_north = [
-        far(cy, near_f.at[2], 6, "gy", gy + 1),
-        far(land, near_i.at[2], 7, "gy", gy + 1),
-        far(spectrum.at[:, pl.ds(cells - 1, 1), :], lat.at[0], 8, "gy", gy + 1),
+        far(cy_h, near_f.at[2], 6, "gy", gy + 1),
+        far(land_h, near_i.at[2], 7, "gy", gy + 1),
+        far(rim.at[1], lat.at[0], 8, "gy", gy + 1),
     ]
     to_south = [
-        far(cy, near_f.at[3], 9, "gy", gy - 1),
-        far(land, near_i.at[3], 10, "gy", gy - 1),
-        far(spectrum.at[:, pl.ds(0, 1), :], lat.at[1], 11, "gy", gy - 1),
+        far(cy_h, near_f.at[3], 9, "gy", gy - 1),
+        far(land_h, near_i.at[3], 10, "gy", gy - 1),
+        far(rim.at[0], lat.at[1], 11, "gy", gy - 1),
     ]
 
     @pl.when(jnp.logical_not(has_south))
@@ -137,14 +150,18 @@
             for copy in to_south[first:last]:
                 copy.wait_recv()
 
+    for copy in to_east[:2] + to_west[:2]:
+        copy.start()
+    each_lat("start", 0, 2)
+    small[0].wait()
+    small[1].wait()
     each_lat("start", 2, 3)
     for copy in to_east[2:] + to_west[2:]:
         copy.start()
-    for copy in to_east[:2] + to_west[:2]:
-        copy.start()
-    each_lat("start", 0, 2)
-
-    freqs = speed.shape[1]
+    for copy in small[2:]:
+        copy.wait()
+
+    freqs = coeffs.shape[2]
     params[...] = jnp.zeros(params.shape, jnp.float32)
     params[0:1, 0:freqs] = speed[...]
     params[1:2, 0:freqs] = growth[...]
@@ -153,12 +170,11 @@
     hot = (spots == lax.broadcasted_iota(jnp.int32, (params.shape[1], bins), 0)).astype(jnp.float32)
     by_bin = jnp.dot(params[...], hot, precision=lax.Precision.HIGHEST, preferred_element_type=jnp.float32)
     cosine, sine = trig[0:1], trig[1:2]
-    table_out[0:1] = by_bin[0:1] * cosine
-    table_out[1:2] = by_bin[0:1] * sine
-    table_out[2:3] = by_bin[1:2] * cosine
-    table_out[3:4] = by_bin[1:2] * sine
-    table_out[4:5] = by_bin[2:3]
-    table = table_out
+    table[0:1] = by_bin[0:1] * cosine
+    table[1:2] = by_bin[0:1] * sine
+    table[2:3] = by_bin[1:2] * cosine
+    table[3:4] = by_bin[1:2] * sine
+    table[4:5] = by_bin[2:3]
 
     for copy in to_east[:2] + to_west[:2]:
         copy.wait_recv()
@@ -205,7 +221,6 @@
     face[6, 0:rows, 0:cells] = sea_of(land[...])
     for k in range(7):
         turned[k] = face[k].T
-    turned_out[...] = turned[0:4, 0:pad]
     spread(pad, stats, turned, 7)
 
     for copy in loads:
@@ -219,8 +234,8 @@
         return courant * jnp.where(courant > 0, sp[f, :, s : s + w], sp[f + 1, :, s : s + w])
 
     lon_send = [
-        far(sens.at[rows - 1], lon_out.at[0], 12, "gx", east),
-        far(sens.at[0], lon_out.at[1], 13, "gx", west),
+        far(sens.at[rows], sens.at[0], 12, "gx", east),
+        far(sens.at[1], sens.at[rows + 1], 13, "gx", west),
     ]
     lat_north = [far(lat_s.at[1, pl.ds(m * half, half)], lat_out.at[0, pl.ds(m * half, half)], 14 + m, "gy", gy + 1) for m in range(2)]
     lat_south = [far(lat_s.at[0, pl.ds(m * half, half)], lat_out.at[1, pl.ds(m * half, half)], 16 + m, "gy", gy - 1) for m in range(2)]
@@ -233,9 +248,6 @@
         @pl.when(has_south)
         def _():
             lat_south[m].start()
-
-    def send_row(i):
-        return pltpu.make_async_copy(sens.at[i], sens_out.at[i], out_sem.at[i])
 
     def row(k, carry):
         i = lax.rem(k + rows - 1, rows)
@@ -283,7 +295,7 @@
             scaled = table[4:5, s : s + w] * advected
             damp = 1.0 + energy[:, 0:w] * scaled
             weighted = adj[i, :, s : s + w] * gain / (damp * damp)
-            sens[i, :, s : s + w] = weighted
+            sens[i + 1, :, s : s + w] = weighted
             term = weighted * scaled * advected
             if w == LANES:
                 total = total + term
@@ -292,20 +304,15 @@
         coupling = (coupling + jnp.sum(total, axis=1, keepdims=True)) * (1.0 / bins)
         coupling = jnp.broadcast_to(coupling, (cells, LANES))
         for s, w in chunks:
-            value = stats[6, i, 0:cells, 0:w] * (sens[i, :, s : s + w] - coupling[:, 0:w])
-            sens[i, :, s : s + w] = value
+            value = stats[6, i, 0:cells, 0:w] * (sens[i + 1, :, s : s + w] - coupling[:, 0:w])
+            sens[i + 1, :, s : s + w] = value
             lat_s[0, i, :, s : s + w] = value[0:1]
             lat_s[1, i, :, s : s + w] = value[cells - 1 : cells]
 
-        @pl.when(k > 0)
-        def _():
-            send_row(lax.rem(k + rows - 2, rows)).start()
-
         return carry
 
     lax.fori_loop(0, rows, row, 0)
     lat_send(1)
-    send_row(rows - 2).start()
 
     fill = [pltpu.make_async_copy(lat.at[m], lat_out.at[m], local_sem.at[m]) for m in range(2)]
     for m, there in ((0, has_south), (1, has_north)):
@@ -338,31 +345,10 @@
         def _(m=m):
             fill[m].wait()
 
-    def finish(i, carry):
-        send_row(i).wait()
-        return carry
-
-    lax.fori_loop(0, rows, finish, 0)
-
-
-def transpose_kernel(
-    sens, lon, lat, turned, table, out,
-    ext, stats, held, done, in_sem, out_sem,
-):
-    rows, cells, bins = sens.shape
+
+def transpose_kernel(ext, lat, stats, table, out, held, done, out_sem):
+    rows, cells, bins = out.shape
     chunks = lane_chunks(bins)
-    pad = stats.shape[2]
-    groups = in_sem.shape[0] - 2
-    size = rows // groups
-    edges = [pltpu.make_async_copy(lon.at[m], ext.at[m * (rows + 1)], in_sem.at[groups + m]) for m in range(2)]
-    part = lambda g: pltpu.make_async_copy(sens.at[pl.ds(g * size, size)], ext.at[pl.ds(g * size + 1, size)], in_sem.at[g])
-    edges[0].start()
-    for g in range(groups):
-        part(g).start()
-    edges[1].start()
-    spread(pad, stats, turned, 4)
-    edges[0].wait()
-    part(0).wait()
 
     def lon_face(f, s, w):
         return stats[0, f, 0:cells, 0:w] * table[0:1, s : s + w] + stats[1, f, 0:cells, 0:w]
@@ -373,14 +359,6 @@
     send = lambda i: pltpu.make_async_copy(done.at[i], out.at[i], out_sem.at[i])
 
     def row(i, carry):
-        @pl.when(jnp.logical_and(lax.rem(i, size) == size - 1, i < rows - 1))
-        def _():
-            part(i // size + 1).wait()
-
-        @pl.when(i == rows - 1)
-        def _():
-            edges[1].wait()
-
         for s, w in chunks:
             own = ext[i + 1, :, s : s + w]
             step = ext[i + 2, :, s : s + w] - own
@@ -411,6 +389,10 @@
     lax.fori_loop(0, rows, finish, 0)
 
 
+def keep(array):
+    return pltpu.with_memory_space_constraint(array, pltpu.HBM)
+
+
 def round_up(value, step):
     return (value + step - 1) // step * step
 
@@ -425,60 +407,57 @@
     f32 = jnp.float32
     dma = pltpu.SemaphoreType.DMA
     shape = jax.ShapeDtypeStruct
-    sens, lon, lat, turned, table = pl.pallas_call(
+    sens, lat, stats, table = pl.pallas_call(
         functools.partial(forward_kernel, nx, ny),
         out_shape=(
-            shape((rows, cells, bins), f32),
-            shape((2, cells, bins), f32),
+            shape((rows + 2, cells, bins), f32),
             shape((2, rows, 1, bins), f32),
-            shape((4, pad, LANES), f32),
+            shape((7, rows + 1, pad, LANES), f32),
             shape((8, bins), f32),
         ),
-        in_specs=[ANY, ANY] + [VMEM] * 10,
-        out_specs=(ANY, ANY, ANY, VMEM, VMEM),
+        in_specs=[HBM] * 12,
+        out_specs=(VMEM,) * 4,
         scratch_shapes=[
             pltpu.VMEM((rows + 2, cells, bins), f32),
             pltpu.VMEM((rows, cells, bins), f32),
-            pltpu.VMEM((rows, cells, bins), f32),
+            pltpu.VMEM((2, rows, 1, bins), f32),
             pltpu.VMEM((2, rows, 1, bins), f32),
             pltpu.VMEM((4, rows, cells), f32),
             pltpu.VMEM((4, rows, cells), jnp.int32),
+            pltpu.VMEM((4, rows, cells), f32),
+            pltpu.VMEM((2, rows, cells), jnp.int32),
+            pltpu.VMEM((3, 1, freqs), f32),
+            pltpu.VMEM((2, bins), f32),
             pltpu.VMEM((8, tall, LANES), f32),
             pltpu.VMEM((7, LANES, LANES), f32),
             pltpu.VMEM((7, LANES, LANES), f32),
-            pltpu.VMEM((7, rows + 1, pad, LANES), f32),
             pltpu.VMEM((cells, bins), f32),
             pltpu.VMEM((cells, bins), f32),
             pltpu.VMEM((2, rows, 1, bins), f32),
             pltpu.VMEM((8, round_up(freqs, 8)), f32),
-            dma((4,)),
-            dma((rows,)),
+            dma((16,)),
             dma((18,)),
             dma((18,)),
         ],
         compiler_params=pltpu.CompilerParams(
-            collective_id=0, has_side_effects=True, vmem_limit_bytes=40 * 2**20
+            collective_id=0, has_side_effects=True, vmem_limit_bytes=24 * 2**20
         ),
         name="forward",
-    )(spectrum, adjoint_in, cx, cy, wx, wy, land, ice,
-      speed.reshape(1, -1), growth.reshape(1, -1), diss.reshape(1, -1), jnp.asarray(trig))
-    groups = max(g for g in (1, 2, 3, 4, 6) if rows % g == 0)
+    )(*map(keep, (spectrum, adjoint_in, cx, cy, wx, wy, land, ice)),
+      *map(keep, (speed.reshape(1, -1), growth.reshape(1, -1), diss.reshape(1, -1), jnp.asarray(trig))))
     return pl.pallas_call(
         transpose_kernel,
         out_shape=shape((rows, cells, bins), f32),
-        in_specs=[ANY, ANY, VMEM, VMEM, VMEM],
-        out_specs=ANY,
+        in_specs=[VMEM] * 4,
+        out_specs=HBM,
         scratch_shapes=[
-            pltpu.VMEM((rows + 2, cells, bins), f32),
-            pltpu.VMEM((4, rows + 1, pad, LANES), f32),
             pltpu.VMEM((cells, bins), f32),
             pltpu.VMEM((rows, cells, bins), f32),
-            dma((groups + 2,)),
             dma((rows,)),
         ],
-        compiler_params=pltpu.CompilerParams(vmem_limit_bytes=32 * 2**20),
+        compiler_params=pltpu.CompilerParams(vmem_limit_bytes=16 * 2**20),
         name="transpose",
-    )(sens, lon, lat, turned, table)
+    )(sens, lat, stats, table)
 
 
 def solution(mesh):

time: 85.5 us -> 32 us (0.37)
  Pallas kernels: 73.4 us -> 31.9 us
  local copies, waits for them, and re-layouts: 11.4 us -> 0 us
    pallas_call x1, Pallas kernels: 52.6 us -> 27.3 us  [body(): pl.pallas_call(functools.partial(forward_kernel, nx, ny), out_shape=(shap...]
    pallas_call x1, Pallas kernels: 20.8 us -> 4.55 us  [body(): pl.pallas_call(transpose_kernel, out_shape=shape((rows, cells, bins), f32...]
    unnamed x24 -> x0, local copies, waits for them, and re-layouts: 11.4 us -> none
where the time goes in v2:
time: 32 us; the launch traced here: 31.9 us
  Pallas kernels  31.9 us (100%)
    pallas_call x1, Pallas kernels, body(): pl.pallas_call(functools.partial(forward_kernel, nx, ny), out_shape=(shap...  27.3 us
    pallas_call x1, Pallas kernels, body(): pl.pallas_call(transpose_kernel, out_shape=shape((rows, cells, bins), f32...  4.55 us

profile of v2, /device:TPU:0, one launch (start us, length us, event | category | flops | bytes accessed | tf_op | source)
XLA Modules:
  0.0 31.9 jit_solution(14594431345842043818)
XLA Ops:
  0.0 27.3 %forward.1 = (f32[26,40,1080]{2,1,0:T(8,128)S(1)}, f32[2,24,1,1080]{3,2,1,0:T(1,128)S(1)}, f32[7,25,48,128]{3,2,1,0:T(8,128)S(1)}, f32[8,1080]{1,0:T(8,128)S(1)}) custom-call(f32[24,40,1080]{2,1,0:T(8,128)} %spectrum.1, f32[24,40,1080]{2,1,0:T(8,128)} %adjoint.1, f32[24,40]{1,0:T(8,128)} %cx_h.1, f32[24,40]{1,0:T(8,128)} %cy_h.1, f32[24,40]{1,0:T(8,128)} %wx_h.1, ...), custom_call_target="tpu_custom_call" | custom-call | tf_op jit(solution)/shard_map/forward/pallas_call | solution.py:410
  27.3 4.5 %transpose.1 = f32[24,40,1080]{2,1,0:T(8,128)} custom-call(f32[26,40,1080]{2,1,0:T(8,128)S(1)} %get-tuple-element.9.ext, f32[2,24,1,1080]{3,2,1,0:T(1,128)S(1)} %get-tuple-element.10.lat, f32[7,25,48,128]{3,2,1,0:T(8,128)S(1)} %get-tuple-element.11.stats, f32[8,1080]{1,0:T(8,128)S(1)} %get-tuple-element.12.table), custom_call_target="tpu_custom_call" | custom-call | tf_op jit(solution)/shard_map/transpose/pallas_call | solution.py:448

commit v3 on v2

--- a/solution.py
+++ b/solution.py
@@ -40,11 +40,11 @@
         stats[k, 0] = jnp.broadcast_to(turned[:, 0:1], (cells, LANES))
 
 
-def forward_kernel(
+def kernel(
     nx, ny,
     spectrum, adjoint, cx_h, cy_h, wx_h, wy_h, land_h, ice_h, speed_h, growth_h, diss_h, trig_h,
-    sens, lat_out, stats, table,
-    sp, adj, lat, rim, near_f, near_i, mine_f, mine_i, coeffs, trig, ext, face, turned, flux, work, lat_s, params,
+    done,
+    sens, lat_out, stats, table, sp, adj, lat, rim, near_f, near_i, mine_f, mine_i, coeffs, trig, ext, face, turned, flux, work, lat_s, params,
     local_sem, far_send, far_recv,
 ):
     gx, gy = lax.axis_index("gx"), lax.axis_index("gy")
@@ -153,11 +153,11 @@
     for copy in to_east[:2] + to_west[:2]:
         copy.start()
     each_lat("start", 0, 2)
+    for copy in to_east[2:] + to_west[2:]:
+        copy.start()
     small[0].wait()
     small[1].wait()
     each_lat("start", 2, 3)
-    for copy in to_east[2:] + to_west[2:]:
-        copy.start()
     for copy in small[2:]:
         copy.wait()
 
@@ -225,8 +225,6 @@
 
     for copy in loads:
         copy.wait()
-    for copy in to_east[2:] + to_west[2:]:
-        copy.wait_recv()
     lat_arrives(2, 3)
 
     def lon_flux(f, s, w):
@@ -249,15 +247,31 @@
         def _():
             lat_south[m].start()
 
+    def lat_done(m):
+        @pl.when(has_north)
+        def _():
+            lat_south[m].wait_recv()
+
+        @pl.when(has_south)
+        def _():
+            lat_north[m].wait_recv()
+
+    early = rows // 3
+
     def row(k, carry):
-        i = lax.rem(k + rows - 1, rows)
-
-        @pl.when(k < 2)
+        i = jnp.where(k < early, k + 1, jnp.where(k == early, 0, jnp.where(k == early + 1, rows - 1, k - 1)))
+
+        @pl.when(k == early)
+        def _():
+            for copy in to_east[2:] + to_west[2:]:
+                copy.wait_recv()
+
+        @pl.when(jnp.logical_or(k == 0, jnp.logical_and(k >= early, k < early + 3)))
         def _():
             for s, w in chunks:
                 flux[:, s : s + w] = lon_flux(i, s, w)
 
-        @pl.when(k == 2)
+        @pl.when(k == early + 3)
         def _():
             for copy in lon_send:
                 copy.start()
@@ -320,73 +334,65 @@
         def _(m=m):
             fill[m].start()
 
-    for copy in to_east + to_west:
-        copy.wait_send()
-    each_lat("wait_send")
-    for copy in lon_send:
-        copy.wait()
-
-    @pl.when(has_north)
-    def _():
-        for copy in lat_north:
-            copy.wait_send()
-        for copy in lat_south:
-            copy.wait_recv()
-
-    @pl.when(has_south)
-    def _():
-        for copy in lat_south:
-            copy.wait_send()
-        for copy in lat_north:
-            copy.wait_recv()
-
     for m, there in ((0, has_south), (1, has_north)):
         @pl.when(jnp.logical_not(there))
         def _(m=m):
             fill[m].wait()
 
-
-def transpose_kernel(ext, lat, stats, table, out, held, done, out_sem):
-    rows, cells, bins = out.shape
-    chunks = lane_chunks(bins)
+    lat_done(0)
 
     def lon_face(f, s, w):
         return stats[0, f, 0:cells, 0:w] * table[0:1, s : s + w] + stats[1, f, 0:cells, 0:w]
 
-    for s, w in chunks:
-        held[:, s : s + w] = jnp.minimum(lon_face(0, s, w), 0.0) * (ext[1, :, s : s + w] - ext[0, :, s : s + w])
-
-    send = lambda i: pltpu.make_async_copy(done.at[i], out.at[i], out_sem.at[i])
-
-    def row(i, carry):
+    def back(k, carry):
+        i = jnp.where(k < rows - 2, k + 1, jnp.where(k == rows - 2, 0, rows - 1))
+
+        @pl.when(k == half - 1)
+        def _():
+            lat_done(1)
+
+        @pl.when(k == rows - 2)
+        def _():
+            for copy in lon_send:
+                copy.wait_recv()
+
+        @pl.when(jnp.logical_or(k == 0, k >= rows - 2))
+        def _():
+            for s, w in chunks:
+                flux[:, s : s + w] = jnp.minimum(lon_face(i, s, w), 0.0) * (
+                    sens[i + 1, :, s : s + w] - sens[i, :, s : s + w]
+                )
+
         for s, w in chunks:
-            own = ext[i + 1, :, s : s + w]
-            step = ext[i + 2, :, s : s + w] - own
+            own = sens[i + 1, :, s : s + w]
+            step = sens[i + 2, :, s : s + w] - own
             courant = lon_face(i + 1, s, w)
-            value = own + held[:, s : s + w] + jnp.maximum(courant, 0.0) * step
-            held[:, s : s + w] = jnp.minimum(courant, 0.0) * step
+            value = own + flux[:, s : s + w] + jnp.maximum(courant, 0.0) * step
+            flux[:, s : s + w] = jnp.minimum(courant, 0.0) * step
             sin_row = table[1:2, s : s + w]
             courant = stats[2, i, 0:cells, 0:w] * sin_row + stats[3, i, 0:cells, 0:w]
-            step = up(own, lat[1, i, :, s : s + w]) - own
+            step = up(own, lat_out[1, i, :, s : s + w]) - own
             value = value + jnp.maximum(courant, 0.0) * step
             low = stats[2, i, cells : cells + 1, 0:w] * sin_row + stats[3, i, cells : cells + 1, 0:w]
-            low = jnp.minimum(low, 0.0) * (own[0:1] - lat[0, i, :, s : s + w])
+            low = jnp.minimum(low, 0.0) * (own[0:1] - lat_out[0, i, :, s : s + w])
             done[i, :, s : s + w] = value + down(jnp.minimum(courant, 0.0) * step, low)
-
-        @pl.when(i > 0)
-        def _():
-            send(i - 1).start()
-
         return carry
 
-    lax.fori_loop(0, rows, row, 0)
-    send(rows - 1).start()
-
-    def finish(i, carry):
-        send(i).wait()
-        return carry
-
-    lax.fori_loop(0, rows, finish, 0)
+    lax.fori_loop(0, rows, back, 0)
+
+    for copy in to_east + to_west + lon_send:
+        copy.wait_send()
+    each_lat("wait_send")
+
+    @pl.when(has_north)
+    def _():
+        for copy in lat_north:
+            copy.wait_send()
+
+    @pl.when(has_south)
+    def _():
+        for copy in lat_south:
+            copy.wait_send()
 
 
 def keep(array):
@@ -407,17 +413,16 @@
     f32 = jnp.float32
     dma = pltpu.SemaphoreType.DMA
     shape = jax.ShapeDtypeStruct
-    sens, lat, stats, table = pl.pallas_call(
-        functools.partial(forward_kernel, nx, ny),
-        out_shape=(
-            shape((rows + 2, cells, bins), f32),
-            shape((2, rows, 1, bins), f32),
-            shape((7, rows + 1, pad, LANES), f32),
-            shape((8, bins), f32),
-        ),
+    return pl.pallas_call(
+        functools.partial(kernel, nx, ny),
+        out_shape=shape((rows, cells, bins), f32),
         in_specs=[HBM] * 12,
-        out_specs=(VMEM,) * 4,
+        out_specs=VMEM,
         scratch_shapes=[
+            pltpu.VMEM((rows + 2, cells, bins), f32),
+            pltpu.VMEM((2, rows, 1, bins), f32),
+            pltpu.VMEM((7, rows + 1, pad, LANES), f32),
+            pltpu.VMEM((8, bins), f32),
             pltpu.VMEM((rows + 2, cells, bins), f32),
             pltpu.VMEM((rows, cells, bins), f32),
             pltpu.VMEM((2, rows, 1, bins), f32),
@@ -440,24 +445,11 @@
             dma((18,)),
         ],
         compiler_params=pltpu.CompilerParams(
-            collective_id=0, has_side_effects=True, vmem_limit_bytes=24 * 2**20
+            collective_id=0, has_side_effects=True, vmem_limit_bytes=36 * 2**20
         ),
-        name="forward",
+        name="step",
     )(*map(keep, (spectrum, adjoint_in, cx, cy, wx, wy, land, ice)),
       *map(keep, (speed.reshape(1, -1), growth.reshape(1, -1), diss.reshape(1, -1), jnp.asarray(trig))))
-    return pl.pallas_call(
-        transpose_kernel,
-        out_shape=shape((rows, cells, bins), f32),
-        in_specs=[VMEM] * 4,
-        out_specs=HBM,
-        scratch_shapes=[
-            pltpu.VMEM((cells, bins), f32),
-            pltpu.VMEM((rows, cells, bins), f32),
-            dma((rows,)),
-        ],
-        compiler_params=pltpu.CompilerParams(vmem_limit_bytes=16 * 2**20),
-        name="transpose",
-    )(sens, lat, stats, table)
 
 
 def solution(mesh):

time: 32 us -> 31.8 us (level)
  Pallas kernels: 31.9 us -> 29.5 us
  local copies, waits for them, and re-layouts: 0 us -> 2.09 us
    pallas_call x2 -> x1, Pallas kernels: 31.9 us -> 29.5 us  [body(): pl.pallas_call(functools.partial(kernel, nx, ny), out_shape=shape((rows,...]
    unnamed x0 -> x1, local copies, waits for them, and re-layouts: none -> 2.09 us
where the time goes in v3:
time: 31.8 us; the launch traced here: 31.6 us
  Pallas kernels  29.5 us (93%)
  local copies, waits for them, and re-layouts  2.09 us (7%)
    pallas_call x1, Pallas kernels, body(): pl.pallas_call(functools.partial(kernel, nx, ny), out_shape=shape((rows,...  29.5 us
    unnamed x1, local copies, waits for them, and re-layouts  2.09 us

profile of v3, /device:TPU:0, one launch (start us, length us, event | category | flops | bytes accessed | tf_op | source)
XLA Modules:
  0.0 31.6 jit_solution(1233968593713834551)
XLA Ops:
  0.0 29.5 %step.1 = f32[24,40,1080]{2,1,0:T(8,128)S(1)} custom-call(f32[24,40,1080]{2,1,0:T(8,128)} %spectrum.1, f32[24,40,1080]{2,1,0:T(8,128)} %adjoint.1, f32[24,40]{1,0:T(8,128)} %cx_h.1, f32[24,40]{1,0:T(8,128)} %cy_h.1, f32[24,40]{1,0:T(8,128)} %wx_h.1, f32[24,40]{1,0:T(8,128)} %wy_h.1, s32[24,40]{1,0:T(8,128)} %land_h.1, s32[24,40]{1,0:T(8,128)} %ice_h.1, ...), custom_call_target="tpu_custom_call" | custom-call | tf_op jit(solution)/shard_map/step/pallas_call | solution.py:416
  29.5 2.1 %copy.14 = f32[24,40,1080]{2,1,0:T(8,128)} copy(f32[24,40,1080]{2,1,0:T(8,128)S(1)} %step.1) | data formatting | bytes 8294400

commit v4 on v3

--- a/solution.py
+++ b/solution.py
@@ -27,17 +27,15 @@
     return jnp.concatenate([first, block[:-1]], axis=0)
 
 
-def spread(cells, stats, table, count):
-    for k in range(count):
-        turned = table[k][:cells, :]
-
-        def one(i, carry, k=k, turned=turned):
-            column = pltpu.roll(turned, LANES - i, axis=1)[:, 0:1]
-            stats[k, i] = jnp.broadcast_to(column, (cells, LANES))
-            return carry
-
-        lax.fori_loop(1, stats.shape[1], one, 0, unroll=4)
-        stats[k, 0] = jnp.broadcast_to(turned[:, 0:1], (cells, LANES))
+def spread(stats, turned, first, last):
+    columns, pad = stats.shape[1:3]
+
+    def one(k, carry):
+        for i in range(columns):
+            stats[k, i] = jnp.broadcast_to(turned[k, 0:pad, i : i + 1], (pad, LANES))
+        return carry
+
+    lax.fori_loop(first, last, one, 0)
 
 
 def kernel(
@@ -88,7 +86,7 @@
                     src.at[pl.ds(m * half, half)], dst.at[pl.ds(m * half + off, half)], local_sem.at[2 * n + m]
                 )
             )
-    for copy in loads:
+    for copy in loads[:2]:
         copy.start()
 
     def far(src, dst, n, axis, where):
@@ -158,6 +156,8 @@
     small[0].wait()
     small[1].wait()
     each_lat("start", 2, 3)
+    for copy in loads[2:]:
+        copy.start()
     for copy in small[2:]:
         copy.wait()
 
@@ -176,11 +176,19 @@
     table[3:4] = by_bin[1:2] * sine
     table[4:5] = by_bin[2:3]
 
+    sea_of = lambda mask: (1 - mask).astype(jnp.float32)
+    face[...] = jnp.zeros(face.shape, jnp.float32)
+    ice_free = sea_of(ice[...])
+    face[4, 0:rows, 0:cells] = wx[...] * ice_free
+    face[5, 0:rows, 0:cells] = wy[...] * ice_free
+    face[6, 0:rows, 0:cells] = sea_of(land[...])
+    for k in range(4, 7):
+        turned[k] = face[k].T
+    spread(stats, turned, 4, 7)
     for copy in to_east[:2] + to_west[:2]:
         copy.wait_recv()
     lat_arrives(0, 2)
     ext[...] = jnp.zeros(ext.shape, jnp.float32)
-    sea_of = lambda mask: (1 - mask).astype(jnp.float32)
     ext[0, 0:1, 0:cells] = near_f[0, rows - 1 : rows]
     ext[0, 1 : rows + 1, 0:cells] = cx[...]
     ext[0, rows + 1 : rows + 2, 0:cells] = near_f[1, 0:1]
@@ -193,7 +201,6 @@
     ext[5, 0:rows, 0:cells] = sea_of(near_i[2])
     ext[6, 0:rows, 0:cells] = near_f[3]
     ext[7, 0:rows, 0:cells] = sea_of(near_i[3])
-    face[...] = jnp.zeros(face.shape, jnp.float32)
     opened = ext[1, 0 : rows + 1] * ext[1, 1 : rows + 2]
     face[0, 0 : rows + 1] = opened
     face[1, 0 : rows + 1] = opened * (0.5 * (ext[0, 0 : rows + 1] + ext[0, 1 : rows + 2]))
@@ -215,13 +222,9 @@
     opened = sea_a * sea_b
     face[2, 0:tall] = jnp.where(closed, 0.0, opened)
     face[3, 0:tall] = jnp.where(closed, 0.0, opened * (0.5 * (cy_a + cy_b)))
-    ice_free = sea_of(ice[...])
-    face[4, 0:rows, 0:cells] = wx[...] * ice_free
-    face[5, 0:rows, 0:cells] = wy[...] * ice_free
-    face[6, 0:rows, 0:cells] = sea_of(land[...])
-    for k in range(7):
+    for k in range(4):
         turned[k] = face[k].T
-    spread(pad, stats, turned, 7)
+    spread(stats, turned, 0, 4)
 
     for copy in loads:
         copy.wait()

time: 31.8 us -> 26.1 us (0.82)
  Pallas kernels: 29.5 us -> 23.8 us
    pallas_call x1, Pallas kernels: 29.5 us -> 23.8 us  [body(): pl.pallas_call(functools.partial(kernel, nx, ny), out_shape=shape((rows,...]
where the time goes in v4:
time: 26.1 us; the launch traced here: 25.9 us
  Pallas kernels  23.8 us (91%)
  local copies, waits for them, and re-layouts  2.09 us (8%)
    pallas_call x1, Pallas kernels, body(): pl.pallas_call(functools.partial(kernel, nx, ny), out_shape=shape((rows,...  23.8 us
    unnamed x1, local copies, waits for them, and re-layouts  2.09 us

profile of v4, /device:TPU:0, one launch (start us, length us, event | category | flops | bytes accessed | tf_op | source)
XLA Modules:
  0.0 25.9 jit_solution(1937889260800529956)
XLA Ops:
  0.0 23.8 %step.1 = f32[24,40,1080]{2,1,0:T(8,128)S(1)} custom-call(f32[24,40,1080]{2,1,0:T(8,128)} %spectrum.1, f32[24,40,1080]{2,1,0:T(8,128)} %adjoint.1, f32[24,40]{1,0:T(8,128)} %cx_h.1, f32[24,40]{1,0:T(8,128)} %cy_h.1, f32[24,40]{1,0:T(8,128)} %wx_h.1, f32[24,40]{1,0:T(8,128)} %wy_h.1, s32[24,40]{1,0:T(8,128)} %land_h.1, s32[24,40]{1,0:T(8,128)} %ice_h.1, ...), custom_call_target="tpu_custom_call" | custom-call | tf_op jit(solution)/shard_map/step/pallas_call | solution.py:419
  23.8 2.1 %copy.14 = f32[24,40,1080]{2,1,0:T(8,128)} copy(f32[24,40,1080]{2,1,0:T(8,128)S(1)} %step.1) | data formatting | bytes 8294400
